TPU v7x, 32 devices: a whole 2x2x4 slice. The times are simulated.
32 devices in a mesh: section: 4 (over y, x), ctx: 8 (over z, core).
Axes of the slice: x: 2, y: 2, z: 4, core: 2. Of those that a mesh axis runs over, the one named last changes fastest.
Arguments:
- queries: bfloat16 [4, 8, 1024, 512], P('section', None, 'ctx'), may hold values from -5 to 5
- keys: bfloat16 [4, 8, 1024, 128], P('section', None, 'ctx'), may hold values from -5 to 5
- values: bfloat16 [4, 8, 1024, 128], P('section', None, 'ctx'), may hold values from -6 to 6
- out_grad: bfloat16 [4, 1024, 512], P('section', 'ctx'), may hold values from -6 to 6
- stretch_ids: int32 [16], P('ctx'), may hold values from 0 to 15, as said below
- stash_slot: int32 [4], P('section'), may hold values from 0 to 7
Outputs:
- passed_grads: bfloat16 [4, 1024, 768], P('section', 'ctx')
Inputs may be any that keep to these rules, and one draw needn't show every extreme that they name: `stretch_ids`: for each sequence, the entries of its 8 row blocks (two a block, blocks in order) are a permutation of 0 to 15 in which a block's two entries are some c and 15 - c, in either order.
All inputs are finite; a program needn't handle non-finite values.
Results may differ from a plain program's by a relative error of at most 0.035.
Values may be sent and summed in bfloat16 or wider, within the bound.
A program may use at most 64 MiB of HBM per device.

v0:
```python
import math

import jax
import jax.numpy as jnp
from jax import lax
from jax.sharding import PartitionSpec as P

SEQS = 1


neg_large = -1e30


def passed_along(value, axis, steps):
    count = lax.axis_size(axis)
    pairs = [(source, (source + steps) % count) for source in range(count)]
    return lax.ppermute(value, axis, pairs)


def token_positions(stretch_numbers, row_count, stretch_size):
    row_ids = jnp.arange(row_count, dtype=jnp.int32)
    matches = (row_ids // stretch_size)[:, None] == jnp.arange(
        stretch_numbers.shape[0], dtype=jnp.int32
    )[None, :]
    stretch_start = jnp.sum(jnp.where(matches, stretch_numbers[None, :], 0), axis=1)
    return stretch_start * stretch_size + row_ids % stretch_size


def block_scores(query_rows, key_block, query_place, key_place, softmax_scale):
    scores = (
        jnp.einsum("thd,cd->thc", query_rows, key_block, preferred_element_type=jnp.float32)
        * softmax_scale
    )
    visible = key_place[None, None, :] <= query_place[:, None, None]
    return (scores, visible)


def forward_block(
    carried, query_rows, key_block, value_block, query_place, key_place, softmax_scale
):
    row_top, row_total, summed = carried
    scores, visible = block_scores(query_rows, key_block, query_place, key_place, softmax_scale)
    new_top = jnp.maximum(row_top, jnp.max(jnp.where(visible, scores, neg_large), axis=2))
    weights = jnp.where(visible, jnp.exp(scores - new_top[:, :, None]), 0.0)
    fading = jnp.exp(row_top - new_top)
    row_total = row_total * fading + jnp.sum(weights, axis=2)
    summed = summed * fading[:, :, None] + jnp.einsum(
        "thc,cd->thd", weights.astype(jnp.bfloat16), value_block, preferred_element_type=jnp.float32
    )
    return (new_top, row_total, summed)


def finish_forward(carried, grad_rows):
    row_top, row_total, summed = carried
    attention = summed / row_total[:, :, None]
    row_delta = jnp.sum(grad_rows.astype(jnp.float32) * attention, axis=2)
    return (row_top + jnp.log(row_total), row_delta)


def backward_block(
    query_rows,
    grad_rows,
    key_block,
    value_block,
    query_place,
    key_place,
    log_total,
    row_delta,
    softmax_scale,
):
    scores, visible = block_scores(query_rows, key_block, query_place, key_place, softmax_scale)
    weights = jnp.where(visible, jnp.exp(scores - log_total[:, :, None]), 0.0)
    probs_half = weights.astype(jnp.bfloat16)
    prob_grad = jnp.einsum(
        "thd,cd->thc", grad_rows, value_block, preferred_element_type=jnp.float32
    )
    score_grad = (softmax_scale * weights * (prob_grad - row_delta[:, :, None])).astype(
        jnp.bfloat16
    )
    query_grad = jnp.einsum(
        "thc,cd->thd", score_grad, key_block, preferred_element_type=jnp.float32
    )
    key_grad = jnp.einsum("thc,thd->cd", score_grad, query_rows, preferred_element_type=jnp.float32)
    value_grad = jnp.einsum(
        "thc,thd->cd", probs_half, grad_rows, preferred_element_type=jnp.float32
    )
    return (query_grad, jnp.concatenate([key_grad, value_grad], axis=1))


def turn_grads(pair_term):
    return passed_along(pair_term.astype(jnp.bfloat16), "ctx", SEQS).astype(pair_term.dtype)


def per_device(queries, keys, values, out_grad, stretch_ids, stash_slot):
    stash_index = stash_slot[0]
    query_flat = lax.dynamic_index_in_dim(queries[0], stash_index, 0, keepdims=False)
    key_rows = lax.dynamic_index_in_dim(keys[0], stash_index, 0, keepdims=False)
    value_rows = lax.dynamic_index_in_dim(values[0], stash_index, 0, keepdims=False)
    row_count, head_size = key_rows.shape
    group_size = query_flat.shape[1] // head_size
    stretch_size = row_count // 2
    softmax_scale = 1.0 / math.sqrt(head_size)
    query_rows = query_flat.reshape(row_count, group_size, head_size)
    grad_rows = out_grad[0].reshape(row_count, group_size, head_size)
    query_place = token_positions(stretch_ids, row_count, stretch_size)
    initial = (
        jnp.full((row_count, group_size), neg_large, jnp.float32),
        jnp.zeros((row_count, group_size), jnp.float32),
        jnp.zeros((row_count, group_size, head_size), jnp.float32),
    )
    own_block = (key_rows, value_rows, stretch_ids)
    span_count = lax.axis_size("ctx") // SEQS

    def block_place(block):
        return token_positions(block[2], row_count, stretch_size)

    def forward_on(carried, block):
        return forward_block(
            carried, query_rows, block[0], block[1], query_place, block_place(block), softmax_scale
        )

    def forward_scan(loop_state, unused):
        carried, block = loop_state
        carried = forward_on(carried, block)
        block = passed_along((block[0], block[1], block[2]), "ctx", SEQS)
        return ((carried, block), block)

    (carried, block), seen = lax.scan(
        forward_scan, (initial, own_block), None, length=span_count - 1
    )
    carried = forward_on(carried, block)
    log_total, row_delta = finish_forward(carried, grad_rows)

    def backward_on(block):
        return backward_block(
            query_rows,
            grad_rows,
            block[0],
            block[1],
            query_place,
            block_place(block),
            log_total,
            row_delta,
            softmax_scale,
        )

    def seen_block(position):
        return jax.tree.map(
            lambda stacked: lax.dynamic_index_in_dim(stacked, position, 0, keepdims=False), seen
        )

    own_grad, own_term = backward_on(own_block)
    query_grad, pair_term = backward_on(seen_block(0))
    query_grad = query_grad + own_grad

    def backward_seen(turn_index, loop_state):
        query_grad, pair_term = loop_state
        grad_part, term_part = backward_on(seen_block(turn_index + 1))
        return (query_grad + grad_part, turn_grads(pair_term) + term_part)

    query_grad, pair_term = lax.fori_loop(0, span_count - 2, backward_seen, (query_grad, pair_term))
    pair_grad = turn_grads(pair_term) + own_term
    message = jnp.concatenate(
        [query_grad.reshape(row_count, group_size * head_size), pair_grad], axis=1
    ).astype(jnp.bfloat16)
    passed = passed_along(message, "section", -1)
    return passed[None]


def solution(mesh):
    in_specs = (
        P("section", None, "ctx", None),
        P("section", None, "ctx", None),
        P("section", None, "ctx", None),
        P("section", "ctx", None),
        P("ctx"),
        P("section"),
    )
    out_specs = P("section", "ctx", None)
    return jax.shard_map(
        per_device, mesh=mesh, in_specs=in_specs, out_specs=out_specs, check_vma=False
    )
```

profile of v0, /device:TPU:0, one launch (start us, length us, event | category | flops | bytes accessed | tf_op | source)
XLA Modules:
  0.0 97.6 jit_solution(16924970269566993945)
XLA Ops:
  0.0 0.7 copy.132
  1.7 0.8 dynamic-slice_bitcast_fusion
  2.5 0.8 dynamic-slice_bitcast_fusion.1
  3.3 42.5 %while.47 = (s32[]{:T(128)}, f32[128,4]{0,1:T(4,128)S(1)}, f32[128,4]{0,1:T(4,128)S(1)}, f32[128,4,128]{2,0,1:T(8,128)S(1)}, bf16[128,128]{1,0:T(8,128)(2,1)S(1)...) while((s32[]{:T(128)}, f32[128,4]{0,1:T(4,128)S(1)}, ...), condition=%wide.region_5.6_spmd.clone, body=%wide.region_1.5_spmd.clone.sunk | while | flops 34362496 | bytes 2133861 | solution.py:128
  3.4 0.5 collective-permute-start.1
  3.9 2.7 %collective-permute-start.2 = (bf16[128,128]{1,0:T(8,128)(2,1)S(1)}, bf16[128,128]{1,0:T(8,128)(2,1)S(1)}, u32[]{:S(2)}, u32[]{:S(2)}) collective-permute-start(bf16[128,128]{1,0:T(8,128)(2,1)S(1)} %copy.105), channel_id=1, source_target_pairs={{0,1},{1,2},{2,3},{3,4},{4,5},{5,6},{6,7},{7,0},{8,9},{9,10},{10,1... | collective-permute-start | bytes 98312 | tf_op jit(solution)/shard_map/while/body/eval_jaxpr/ppermute | solution.py:17
  7.2 0.3 convolution_add_fusion.7
  7.5 3.9 %collective-permute-done.3 = s32[2]{0:T(128)S(1)} collective-permute-done((s32[2]{0:T(128)S(1)}, s32[2]{0:T(128)S(1)}, u32[]{:S(2)}, u32[]{:S(2)}) %collective-permute-start.3) | collective-permute-done | bytes 40 | tf_op jit(solution)/shard_map/while/body/eval_jaxpr/ppermute | solution.py:17
  12.2 0.3 convolution_add_fusion.7
  12.5 4.6 %collective-permute-done.3 = s32[2]{0:T(128)S(1)} collective-permute-done((s32[2]{0:T(128)S(1)}, s32[2]{0:T(128)S(1)}, u32[]{:S(2)}, u32[]{:S(2)}) %collective-permute-start.3) | collective-permute-done | bytes 40 | tf_op jit(solution)/shard_map/while/body/eval_jaxpr/ppermute | solution.py:17
  18.2 4.6 %collective-permute-done.3 = s32[2]{0:T(128)S(1)} collective-permute-done((s32[2]{0:T(128)S(1)}, s32[2]{0:T(128)S(1)}, u32[]{:S(2)}, u32[]{:S(2)}) %collective-permute-start.3) | collective-permute-done | bytes 40 | tf_op jit(solution)/shard_map/while/body/eval_jaxpr/ppermute | solution.py:17
  24.0 4.6 %collective-permute-done.3 = s32[2]{0:T(128)S(1)} collective-permute-done((s32[2]{0:T(128)S(1)}, s32[2]{0:T(128)S(1)}, u32[]{:S(2)}, u32[]{:S(2)}) %collective-permute-start.3) | collective-permute-done | bytes 40 | tf_op jit(solution)/shard_map/while/body/eval_jaxpr/ppermute | solution.py:17
  29.7 4.6 %collective-permute-done.3 = s32[2]{0:T(128)S(1)} collective-permute-done((s32[2]{0:T(128)S(1)}, s32[2]{0:T(128)S(1)}, u32[]{:S(2)}, u32[]{:S(2)}) %collective-permute-start.3) | collective-permute-done | bytes 40 | tf_op jit(solution)/shard_map/while/body/eval_jaxpr/ppermute | solution.py:17
  35.4 4.6 %collective-permute-done.3 = s32[2]{0:T(128)S(1)} collective-permute-done((s32[2]{0:T(128)S(1)}, s32[2]{0:T(128)S(1)}, u32[]{:S(2)}, u32[]{:S(2)}) %collective-permute-start.3) | collective-permute-done | bytes 40 | tf_op jit(solution)/shard_map/while/body/eval_jaxpr/ppermute | solution.py:17
  41.2 4.6 %collective-permute-done.3 = s32[2]{0:T(128)S(1)} collective-permute-done((s32[2]{0:T(128)S(1)}, s32[2]{0:T(128)S(1)}, u32[]{:S(2)}, u32[]{:S(2)}) %collective-permute-start.3) | collective-permute-done | bytes 40 | tf_op jit(solution)/shard_map/while/body/eval_jaxpr/ppermute | solution.py:17
  46.0 0.8 copy-done.1
  47.1 0.3 select_reduce_fusion.1
  48.2 0.3 fusion.46
  49.1 1.0 %fusion.36 = f32[128,4,128]{2,0,1:T(8,128)S(1)} fusion(bf16[128,4,128]{0,2,1:T(8,128)(2,1)S(1)} %bitcast.174, f32[128,4]{0,1:T(4,128)S(1)} %get-tuple-element.778, pred[128,128]{1,0:T(8,128)(4,1)S(1)} %get-tuple-element.576, bf16[1,8,128,128]{3,2,1,0:T(8,128)(2,1)} %param.11, s32[]{:T(128)S(6)} %select_n.194), kind=kOutput, calls=%fused_computation.69 | convolution fusion | flops 16973824 | bytes 444420 | tf_op jit(solution)/shard_map/thd,cd->thc/dot_general | solution.py:31
  50.1 1.0 %fusion.45 = bf16[128,4,128]{2,0,1:T(8,128)(2,1)S(1)} fusion(bf16[128,4,128]{0,2,1:T(8,128)(2,1)S(1)} %bitcast.168, f32[128,4,128]{2,0,1:T(8,128)S(1)} %fusion.36, f32[128,4]{0,1:T(4,128)S(1)} %fusion.46, bf16[1,8,128,128]{3,2,1,0:T(8,128)(2,1)} %param.12, s32[]{:T(128)S(6)} %select_n.194), kind=kOutput, calls=%fused_computation.82 | convolution fusion | flops 17039360 | bytes 559108 | tf_op jit(solution)/shard_map/thd,cd->thc/dot_general | solution.py:74
  51.1 0.9 convolution_add_fusion.2
  52.1 33.5 %while.46 = (s32[]{:T(128)}, f32[128,4,128]{2,0,1:T(8,128)S(1)}, bf16[128,256]{0,1:T(8,128)(2,1)S(1)}, s32[7,2]{1,0:T(8,128)S(1)}, s32[128]{0:T(128)S(1)}, /*ind...) while((s32[]{:T(128)}, f32[128,4,128]{2,0,1:T(8,128)S(1)}, ...), condition=%wide.region_13.14_spmd, body=%wide.region_11.13_spmd.sunk | while | flops 84626048 | bytes 3022591 | solution.py:161
  53.4 4.2 %collective-permute-done = bf16[128,256]{0,1:T(8,128)(2,1)S(1)} collective-permute-done((bf16[128,256]{0,1:T(8,128)(2,1)S(1)}, bf16[128,256]{0,1:T(8,128)(2,1)S(1)}, u32[]{:S(2)}, u32[]{:S(2)}) %collective-permute-start) | collective-permute-done | bytes 65568 | tf_op jit(solution)/shard_map/while/body/eval_jaxpr/ppermute | solution.py:17
  59.0 4.2 %collective-permute-done = bf16[128,256]{0,1:T(8,128)(2,1)S(1)} collective-permute-done((bf16[128,256]{0,1:T(8,128)(2,1)S(1)}, bf16[128,256]{0,1:T(8,128)(2,1)S(1)}, u32[]{:S(2)}, u32[]{:S(2)}) %collective-permute-start) | collective-permute-done | bytes 65568 | tf_op jit(solution)/shard_map/while/body/eval_jaxpr/ppermute | solution.py:17
  64.5 4.2 %collective-permute-done = bf16[128,256]{0,1:T(8,128)(2,1)S(1)} collective-permute-done((bf16[128,256]{0,1:T(8,128)(2,1)S(1)}, bf16[128,256]{0,1:T(8,128)(2,1)S(1)}, u32[]{:S(2)}, u32[]{:S(2)}) %collective-permute-start) | collective-permute-done | bytes 65568 | tf_op jit(solution)/shard_map/while/body/eval_jaxpr/ppermute | solution.py:17
  70.1 4.2 %collective-permute-done = bf16[128,256]{0,1:T(8,128)(2,1)S(1)} collective-permute-done((bf16[128,256]{0,1:T(8,128)(2,1)S(1)}, bf16[128,256]{0,1:T(8,128)(2,1)S(1)}, u32[]{:S(2)}, u32[]{:S(2)}) %collective-permute-start) | collective-permute-done | bytes 65568 | tf_op jit(solution)/shard_map/while/body/eval_jaxpr/ppermute | solution.py:17
  75.7 4.2 %collective-permute-done = bf16[128,256]{0,1:T(8,128)(2,1)S(1)} collective-permute-done((bf16[128,256]{0,1:T(8,128)(2,1)S(1)}, bf16[128,256]{0,1:T(8,128)(2,1)S(1)}, u32[]{:S(2)}, u32[]{:S(2)}) %collective-permute-start) | collective-permute-done | bytes 65568 | tf_op jit(solution)/shard_map/while/body/eval_jaxpr/ppermute | solution.py:17
  81.3 4.2 %collective-permute-done = bf16[128,256]{0,1:T(8,128)(2,1)S(1)} collective-permute-done((bf16[128,256]{0,1:T(8,128)(2,1)S(1)}, bf16[128,256]{0,1:T(8,128)(2,1)S(1)}, u32[]{:S(2)}, u32[]{:S(2)}) %collective-permute-start) | collective-permute-done | bytes 65568 | tf_op jit(solution)/shard_map/while/body/eval_jaxpr/ppermute | solution.py:17
  86.0 5.1 %collective-permute-done.4 = bf16[128,256]{0,1:T(8,128)(2,1)S(1)} collective-permute-done((bf16[128,256]{0,1:T(8,128)(2,1)S(1)}, bf16[128,256]{0,1:T(8,128)(2,1)S(1)}, u32[]{:S(2)}, u32[]{:S(2)}) %collective-permute-start.4) | collective-permute-done | bytes 65568 | tf_op jit(solution)/shard_map/ppermute | solution.py:17
  91.2 2.5 %collective-permute-start.5 = (bf16[128,768]{1,0:T(8,128)(2,1)S(1)}, bf16[128,768]{1,0:T(8,128)(2,1)S(1)}, u32[]{:S(2)}, u32[]{:S(2)}) collective-permute-start(bf16[128,768]{1,0:T(8,128)(2,1)S(1)} %pad_maximum_fusion), channel_id=1, source_target_pairs={{0,24},{8,0},{16,8},{24,16},{1,25},{9,1},{17,9},{25,17},{2,26},{10... | collective-permute-start | bytes 589832 | tf_op jit(solution)/shard_map/ppermute | solution.py:17
  93.7 3.2 %collective-permute-done.5 = bf16[128,768]{1,0:T(8,128)(2,1)S(1)} collective-permute-done((bf16[128,768]{1,0:T(8,128)(2,1)S(1)}, bf16[128,768]{1,0:T(8,128)(2,1)S(1)}, u32[]{:S(2)}, u32[]{:S(2)}) %collective-permute-start.5) | collective-permute-done | bytes 196640 | tf_op jit(solution)/shard_map/ppermute | solution.py:17
  97.0 0.7 copy.133
  (252 shorter events, 16.5 us)
Async XLA Ops:
  0.0 1.4 %copy-start = (bf16[1,8,128,512]{3,2,1,0:T(8,128)(2,1)S(1)}, bf16[1,8,128,512]{3,2,1,0:T(8,128)(2,1)}, u32[]{:S(2)}) copy-start(bf16[1,8,128,512]{3,2,1,0:T(8,128)(2,1)} %param.10) | copy-start | bytes 3145732
  3.4 8.0 %collective-permute-start.1 = (bf16[128,128]{1,0:T(8,128)(2,1)S(1)}, bf16[128,128]{1,0:T(8,128)(2,1)S(1)}, u32[]{:S(2)}, u32[]{:S(2)}) collective-permute-start(bf16[128,128]{1,0:T(8,128)(2,1)S(1)} %copy.104), channel_id=1, source_target_pairs={{0,1},{1,2},{2,3},{3,4},{4,5},{5,6},{6,7},{7,0},{8,9},{9,10},{10,1... | collective-permute-start | bytes 98312 | tf_op jit(solution)/shard_map/while/body/eval_jaxpr/ppermute | solution.py:17
  3.9 7.5 %collective-permute-start.2 = (bf16[128,128]{1,0:T(8,128)(2,1)S(1)}, bf16[128,128]{1,0:T(8,128)(2,1)S(1)}, u32[]{:S(2)}, u32[]{:S(2)}) collective-permute-start(bf16[128,128]{1,0:T(8,128)(2,1)S(1)} %copy.105), channel_id=1, source_target_pairs={{0,1},{1,2},{2,3},{3,4},{4,5},{5,6},{6,7},{7,0},{8,9},{9,10},{10,1... | collective-permute-start | bytes 98312 | tf_op jit(solution)/shard_map/while/body/eval_jaxpr/ppermute | solution.py:17
  6.6 4.8 %collective-permute-start.3 = (s32[2]{0:T(128)S(1)}, s32[2]{0:T(128)S(1)}, u32[]{:S(2)}, u32[]{:S(2)}) collective-permute-start(s32[2]{0:T(128)S(1)} %copy.106), channel_id=1, source_target_pairs={{0,1},{1,2},{2,3},{3,4},{4,5},{5,6},{6,7},{7,0},{8,9},{9,10},{10,1... | collective-permute-start | bytes 32 | tf_op jit(solution)/shard_map/while/body/eval_jaxpr/ppermute | solution.py:17
  11.5 5.7 %collective-permute-start.1 = (bf16[128,128]{1,0:T(8,128)(2,1)S(1)}, bf16[128,128]{1,0:T(8,128)(2,1)S(1)}, u32[]{:S(2)}, u32[]{:S(2)}) collective-permute-start(bf16[128,128]{1,0:T(8,128)(2,1)S(1)} %copy.104), channel_id=1, source_target_pairs={{0,1},{1,2},{2,3},{3,4},{4,5},{5,6},{6,7},{7,0},{8,9},{9,10},{10,1... | collective-permute-start | bytes 98312 | tf_op jit(solution)/shard_map/while/body/eval_jaxpr/ppermute | solution.py:17
  11.6 5.6 %collective-permute-start.2 = (bf16[128,128]{1,0:T(8,128)(2,1)S(1)}, bf16[128,128]{1,0:T(8,128)(2,1)S(1)}, u32[]{:S(2)}, u32[]{:S(2)}) collective-permute-start(bf16[128,128]{1,0:T(8,128)(2,1)S(1)} %copy.105), channel_id=1, source_target_pairs={{0,1},{1,2},{2,3},{3,4},{4,5},{5,6},{6,7},{7,0},{8,9},{9,10},{10,1... | collective-permute-start | bytes 98312 | tf_op jit(solution)/shard_map/while/body/eval_jaxpr/ppermute | solution.py:17
  11.6 5.5 %collective-permute-start.3 = (s32[2]{0:T(128)S(1)}, s32[2]{0:T(128)S(1)}, u32[]{:S(2)}, u32[]{:S(2)}) collective-permute-start(s32[2]{0:T(128)S(1)} %copy.106), channel_id=1, source_target_pairs={{0,1},{1,2},{2,3},{3,4},{4,5},{5,6},{6,7},{7,0},{8,9},{9,10},{10,1... | collective-permute-start | bytes 32 | tf_op jit(solution)/shard_map/while/body/eval_jaxpr/ppermute | solution.py:17
  17.2 5.7 %collective-permute-start.1 = (bf16[128,128]{1,0:T(8,128)(2,1)S(1)}, bf16[128,128]{1,0:T(8,128)(2,1)S(1)}, u32[]{:S(2)}, u32[]{:S(2)}) collective-permute-start(bf16[128,128]{1,0:T(8,128)(2,1)S(1)} %copy.104), channel_id=1, source_target_pairs={{0,1},{1,2},{2,3},{3,4},{4,5},{5,6},{6,7},{7,0},{8,9},{9,10},{10,1... | collective-permute-start | bytes 98312 | tf_op jit(solution)/shard_map/while/body/eval_jaxpr/ppermute | solution.py:17
  17.3 5.6 %collective-permute-start.2 = (bf16[128,128]{1,0:T(8,128)(2,1)S(1)}, bf16[128,128]{1,0:T(8,128)(2,1)S(1)}, u32[]{:S(2)}, u32[]{:S(2)}) collective-permute-start(bf16[128,128]{1,0:T(8,128)(2,1)S(1)} %copy.105), channel_id=1, source_target_pairs={{0,1},{1,2},{2,3},{3,4},{4,5},{5,6},{6,7},{7,0},{8,9},{9,10},{10,1... | collective-permute-start | bytes 98312 | tf_op jit(solution)/shard_map/while/body/eval_jaxpr/ppermute | solution.py:17
  17.4 5.5 %collective-permute-start.3 = (s32[2]{0:T(128)S(1)}, s32[2]{0:T(128)S(1)}, u32[]{:S(2)}, u32[]{:S(2)}) collective-permute-start(s32[2]{0:T(128)S(1)} %copy.106), channel_id=1, source_target_pairs={{0,1},{1,2},{2,3},{3,4},{4,5},{5,6},{6,7},{7,0},{8,9},{9,10},{10,1... | collective-permute-start | bytes 32 | tf_op jit(solution)/shard_map/while/body/eval_jaxpr/ppermute | solution.py:17
  22.9 5.7 %collective-permute-start.1 = (bf16[128,128]{1,0:T(8,128)(2,1)S(1)}, bf16[128,128]{1,0:T(8,128)(2,1)S(1)}, u32[]{:S(2)}, u32[]{:S(2)}) collective-permute-start(bf16[128,128]{1,0:T(8,128)(2,1)S(1)} %copy.104), channel_id=1, source_target_pairs={{0,1},{1,2},{2,3},{3,4},{4,5},{5,6},{6,7},{7,0},{8,9},{9,10},{10,1... | collective-permute-start | bytes 98312 | tf_op jit(solution)/shard_map/while/body/eval_jaxpr/ppermute | solution.py:17
  23.0 5.6 %collective-permute-start.2 = (bf16[128,128]{1,0:T(8,128)(2,1)S(1)}, bf16[128,128]{1,0:T(8,128)(2,1)S(1)}, u32[]{:S(2)}, u32[]{:S(2)}) collective-permute-start(bf16[128,128]{1,0:T(8,128)(2,1)S(1)} %copy.105), channel_id=1, source_target_pairs={{0,1},{1,2},{2,3},{3,4},{4,5},{5,6},{6,7},{7,0},{8,9},{9,10},{10,1... | collective-permute-start | bytes 98312 | tf_op jit(solution)/shard_map/while/body/eval_jaxpr/ppermute | solution.py:17
  23.1 5.5 %collective-permute-start.3 = (s32[2]{0:T(128)S(1)}, s32[2]{0:T(128)S(1)}, u32[]{:S(2)}, u32[]{:S(2)}) collective-permute-start(s32[2]{0:T(128)S(1)} %copy.106), channel_id=1, source_target_pairs={{0,1},{1,2},{2,3},{3,4},{4,5},{5,6},{6,7},{7,0},{8,9},{9,10},{10,1... | collective-permute-start | bytes 32 | tf_op jit(solution)/shard_map/while/body/eval_jaxpr/ppermute | solution.py:17
  28.7 5.7 %collective-permute-start.1 = (bf16[128,128]{1,0:T(8,128)(2,1)S(1)}, bf16[128,128]{1,0:T(8,128)(2,1)S(1)}, u32[]{:S(2)}, u32[]{:S(2)}) collective-permute-start(bf16[128,128]{1,0:T(8,128)(2,1)S(1)} %copy.104), channel_id=1, source_target_pairs={{0,1},{1,2},{2,3},{3,4},{4,5},{5,6},{6,7},{7,0},{8,9},{9,10},{10,1... | collective-permute-start | bytes 98312 | tf_op jit(solution)/shard_map/while/body/eval_jaxpr/ppermute | solution.py:17
  28.8 5.6 %collective-permute-start.2 = (bf16[128,128]{1,0:T(8,128)(2,1)S(1)}, bf16[128,128]{1,0:T(8,128)(2,1)S(1)}, u32[]{:S(2)}, u32[]{:S(2)}) collective-permute-start(bf16[128,128]{1,0:T(8,128)(2,1)S(1)} %copy.105), channel_id=1, source_target_pairs={{0,1},{1,2},{2,3},{3,4},{4,5},{5,6},{6,7},{7,0},{8,9},{9,10},{10,1... | collective-permute-start | bytes 98312 | tf_op jit(solution)/shard_map/while/body/eval_jaxpr/ppermute | solution.py:17
  28.8 5.5 %collective-permute-start.3 = (s32[2]{0:T(128)S(1)}, s32[2]{0:T(128)S(1)}, u32[]{:S(2)}, u32[]{:S(2)}) collective-permute-start(s32[2]{0:T(128)S(1)} %copy.106), channel_id=1, source_target_pairs={{0,1},{1,2},{2,3},{3,4},{4,5},{5,6},{6,7},{7,0},{8,9},{9,10},{10,1... | collective-permute-start | bytes 32 | tf_op jit(solution)/shard_map/while/body/eval_jaxpr/ppermute | solution.py:17
  34.4 5.7 %collective-permute-start.1 = (bf16[128,128]{1,0:T(8,128)(2,1)S(1)}, bf16[128,128]{1,0:T(8,128)(2,1)S(1)}, u32[]{:S(2)}, u32[]{:S(2)}) collective-permute-start(bf16[128,128]{1,0:T(8,128)(2,1)S(1)} %copy.104), channel_id=1, source_target_pairs={{0,1},{1,2},{2,3},{3,4},{4,5},{5,6},{6,7},{7,0},{8,9},{9,10},{10,1... | collective-permute-start | bytes 98312 | tf_op jit(solution)/shard_map/while/body/eval_jaxpr/ppermute | solution.py:17
  34.5 5.6 %collective-permute-start.2 = (bf16[128,128]{1,0:T(8,128)(2,1)S(1)}, bf16[128,128]{1,0:T(8,128)(2,1)S(1)}, u32[]{:S(2)}, u32[]{:S(2)}) collective-permute-start(bf16[128,128]{1,0:T(8,128)(2,1)S(1)} %copy.105), channel_id=1, source_target_pairs={{0,1},{1,2},{2,3},{3,4},{4,5},{5,6},{6,7},{7,0},{8,9},{9,10},{10,1... | collective-permute-start | bytes 98312 | tf_op jit(solution)/shard_map/while/body/eval_jaxpr/ppermute | solution.py:17
  34.6 5.5 %collective-permute-start.3 = (s32[2]{0:T(128)S(1)}, s32[2]{0:T(128)S(1)}, u32[]{:S(2)}, u32[]{:S(2)}) collective-permute-start(s32[2]{0:T(128)S(1)} %copy.106), channel_id=1, source_target_pairs={{0,1},{1,2},{2,3},{3,4},{4,5},{5,6},{6,7},{7,0},{8,9},{9,10},{10,1... | collective-permute-start | bytes 32 | tf_op jit(solution)/shard_map/while/body/eval_jaxpr/ppermute | solution.py:17
  40.1 5.7 %collective-permute-start.1 = (bf16[128,128]{1,0:T(8,128)(2,1)S(1)}, bf16[128,128]{1,0:T(8,128)(2,1)S(1)}, u32[]{:S(2)}, u32[]{:S(2)}) collective-permute-start(bf16[128,128]{1,0:T(8,128)(2,1)S(1)} %copy.104), channel_id=1, source_target_pairs={{0,1},{1,2},{2,3},{3,4},{4,5},{5,6},{6,7},{7,0},{8,9},{9,10},{10,1... | collective-permute-start | bytes 98312 | tf_op jit(solution)/shard_map/while/body/eval_jaxpr/ppermute | solution.py:17
  40.2 5.6 %collective-permute-start.2 = (bf16[128,128]{1,0:T(8,128)(2,1)S(1)}, bf16[128,128]{1,0:T(8,128)(2,1)S(1)}, u32[]{:S(2)}, u32[]{:S(2)}) collective-permute-start(bf16[128,128]{1,0:T(8,128)(2,1)S(1)} %copy.105), channel_id=1, source_target_pairs={{0,1},{1,2},{2,3},{3,4},{4,5},{5,6},{6,7},{7,0},{8,9},{9,10},{10,1... | collective-permute-start | bytes 98312 | tf_op jit(solution)/shard_map/while/body/eval_jaxpr/ppermute | solution.py:17
  40.3 5.5 %collective-permute-start.3 = (s32[2]{0:T(128)S(1)}, s32[2]{0:T(128)S(1)}, u32[]{:S(2)}, u32[]{:S(2)}) collective-permute-start(s32[2]{0:T(128)S(1)} %copy.106), channel_id=1, source_target_pairs={{0,1},{1,2},{2,3},{3,4},{4,5},{5,6},{6,7},{7,0},{8,9},{9,10},{10,1... | collective-permute-start | bytes 32 | tf_op jit(solution)/shard_map/while/body/eval_jaxpr/ppermute | solution.py:17
  45.9 0.9 copy-start.1
  52.1 5.5 %collective-permute-start = (bf16[128,256]{0,1:T(8,128)(2,1)S(1)}, bf16[128,256]{0,1:T(8,128)(2,1)S(1)}, u32[]{:S(2)}, u32[]{:S(2)}) collective-permute-start(bf16[128,256]{0,1:T(8,128)(2,1)S(1)} %get-tuple-element.787), channel_id=1, source_target_pairs={{0,1},{1,2},{2,3},{3,4},{4,5},{5,6},{6,7},{7,0},{8,9},{9,10},{10,1... | collective-permute-start | bytes 196616 | tf_op jit(solution)/shard_map/while/body/eval_jaxpr/ppermute | solution.py:17
  57.7 5.5 %collective-permute-start = (bf16[128,256]{0,1:T(8,128)(2,1)S(1)}, bf16[128,256]{0,1:T(8,128)(2,1)S(1)}, u32[]{:S(2)}, u32[]{:S(2)}) collective-permute-start(bf16[128,256]{0,1:T(8,128)(2,1)S(1)} %get-tuple-element.787), channel_id=1, source_target_pairs={{0,1},{1,2},{2,3},{3,4},{4,5},{5,6},{6,7},{7,0},{8,9},{9,10},{10,1... | collective-permute-start | bytes 196616 | tf_op jit(solution)/shard_map/while/body/eval_jaxpr/ppermute | solution.py:17
  63.2 5.5 %collective-permute-start = (bf16[128,256]{0,1:T(8,128)(2,1)S(1)}, bf16[128,256]{0,1:T(8,128)(2,1)S(1)}, u32[]{:S(2)}, u32[]{:S(2)}) collective-permute-start(bf16[128,256]{0,1:T(8,128)(2,1)S(1)} %get-tuple-element.787), channel_id=1, source_target_pairs={{0,1},{1,2},{2,3},{3,4},{4,5},{5,6},{6,7},{7,0},{8,9},{9,10},{10,1... | collective-permute-start | bytes 196616 | tf_op jit(solution)/shard_map/while/body/eval_jaxpr/ppermute | solution.py:17
  68.8 5.5 %collective-permute-start = (bf16[128,256]{0,1:T(8,128)(2,1)S(1)}, bf16[128,256]{0,1:T(8,128)(2,1)S(1)}, u32[]{:S(2)}, u32[]{:S(2)}) collective-permute-start(bf16[128,256]{0,1:T(8,128)(2,1)S(1)} %get-tuple-element.787), channel_id=1, source_target_pairs={{0,1},{1,2},{2,3},{3,4},{4,5},{5,6},{6,7},{7,0},{8,9},{9,10},{10,1... | collective-permute-start | bytes 196616 | tf_op jit(solution)/shard_map/while/body/eval_jaxpr/ppermute | solution.py:17
  74.4 5.5 %collective-permute-start = (bf16[128,256]{0,1:T(8,128)(2,1)S(1)}, bf16[128,256]{0,1:T(8,128)(2,1)S(1)}, u32[]{:S(2)}, u32[]{:S(2)}) collective-permute-start(bf16[128,256]{0,1:T(8,128)(2,1)S(1)} %get-tuple-element.787), channel_id=1, source_target_pairs={{0,1},{1,2},{2,3},{3,4},{4,5},{5,6},{6,7},{7,0},{8,9},{9,10},{10,1... | collective-permute-start | bytes 196616 | tf_op jit(solution)/shard_map/while/body/eval_jaxpr/ppermute | solution.py:17
  80.0 5.5 %collective-permute-start = (bf16[128,256]{0,1:T(8,128)(2,1)S(1)}, bf16[128,256]{0,1:T(8,128)(2,1)S(1)}, u32[]{:S(2)}, u32[]{:S(2)}) collective-permute-start(bf16[128,256]{0,1:T(8,128)(2,1)S(1)} %get-tuple-element.787), channel_id=1, source_target_pairs={{0,1},{1,2},{2,3},{3,4},{4,5},{5,6},{6,7},{7,0},{8,9},{9,10},{10,1... | collective-permute-start | bytes 196616 | tf_op jit(solution)/shard_map/while/body/eval_jaxpr/ppermute | solution.py:17
  85.5 5.5 %collective-permute-start.4 = (bf16[128,256]{0,1:T(8,128)(2,1)S(1)}, bf16[128,256]{0,1:T(8,128)(2,1)S(1)}, u32[]{:S(2)}, u32[]{:S(2)}) collective-permute-start(bf16[128,256]{0,1:T(8,128)(2,1)S(1)} %get-tuple-element.444), channel_id=1, source_target_pairs={{0,1},{1,2},{2,3},{3,4},{4,5},{5,6},{6,7},{7,0},{8,9},{9,10},{10,1... | collective-permute-start | bytes 196616 | tf_op jit(solution)/shard_map/ppermute | solution.py:17
  91.2 5.7 %collective-permute-start.5 = (bf16[128,768]{1,0:T(8,128)(2,1)S(1)}, bf16[128,768]{1,0:T(8,128)(2,1)S(1)}, u32[]{:S(2)}, u32[]{:S(2)}) collective-permute-start(bf16[128,768]{1,0:T(8,128)(2,1)S(1)} %pad_maximum_fusion), channel_id=1, source_target_pairs={{0,24},{8,0},{16,8},{24,16},{1,25},{9,1},{17,9},{25,17},{2,26},{10... | collective-permute-start | bytes 589832 | tf_op jit(solution)/shard_map/ppermute | solution.py:17
where the time goes:
time: 98.1 us; the launch traced here: 97.6 us
  waiting for transfers between devices  65.3 us (67%)
  matrix products  14.2 us (14%)
  starting transfers between devices  7.24 us (7%)
  local copies, waits for them, and re-layouts  4.85 us (5%)
  other arithmetic  3.73 us (4%)
  loops' own time  1.43 us (1%)
    ppermute x29, waiting for transfers between devices, passed_along(): return lax.ppermute(value, axis, pairs)  65.3 us
    ppermute x29, starting transfers between devices, passed_along(): return lax.ppermute(value, axis, pairs)  7.24 us
    dot_general x16, matrix products, block_scores(): jnp.einsum('thd,cd->thc', query_rows, key_block, preferred_element_type=j...  4.17 us
    unnamed x9, local copies, waits for them, and re-layouts  2.56 us
    dot_general x8, matrix products, backward_block(): jnp.einsum('thc,cd->thd', score_grad, key_block, preferred_element_type=j...  2.46 us
    dot_general x8, matrix products, backward_block(): jnp.einsum('thd,cd->thc', grad_rows, value_block, preferred_element_type=...  2.31 us
    dot_general x8, matrix products, forward_block(): jnp.einsum('thc,cd->thd', weights.astype(jnp.bfloat16), value_block, pref...  2.3 us
  transfers between devices with their start and end apart: 29, of which 15 were waited for; matrix products, arithmetic and copies ran while one was open for 13% of the time, Pallas kernels for 0%

commit v1 on v0

v1 whole, which is shorter than its diff:
```python
import functools
import math

import jax
import jax.numpy as jnp
from jax import lax
from jax.experimental import pallas as pl
from jax.experimental.pallas import tpu as pltpu
from jax.sharding import PartitionSpec as P

MESH = pl.DeviceIdType.MESH
LOG2E = 1.4426950408889634
hidden = -1e30


def dot(a, b, dims):
    return lax.dot_general(a, b, (dims, ((), ())), preferred_element_type=jnp.float32)


def paired_chip(chip, offset, chips):
    if chips & (chips - 1):
        return lax.rem(2 * chips + offset - chip, chips)
    result = chip
    bit = 1
    while bit < chips:
        result = result + ((offset // bit) % 2) * bit * (1 - 2 * ((chip // bit) % 2))
        bit *= 2
    return result


def over(count, body, backwards=False):
    if count <= 4:
        for step in reversed(range(count)) if backwards else range(count):
            body(step)
    else:
        lax.fori_loop(
            0, count, lambda i, c: (body(count - 1 - i if backwards else i), c)[1], 0
        )


def kernel(
    n,
    sections,
    kv_ref,
    q_hbm,
    g_hbm,
    out_ref,
    q_in,
    g_in,
    q_rows,
    g_rows,
    q_turned,
    g_turned,
    kv_all,
    exps,
    dprobs,
    tops,
    row_top,
    row_total,
    row_delta,
    dq_turned,
    own_part,
    pair_send,
    pair_recv,
    sum_send,
    sum_recv,
    message,
    load_sem,
    kv_send_sem,
    kv_pass_sem,
    kv_recv_sem,
    pair_send_sem,
    pair_recv_sem,
    sum_send_sem,
    sum_recv_sem,
    relay_send_sem,
    relay_recv_sem,
):
    chips = n // 2
    rows = kv_ref.shape[0] - 16
    head = kv_ref.shape[1] // 2
    group = q_hbm.shape[1] // head
    half = rows // 2
    scale = 1.0 / math.sqrt(head)
    me = lax.axis_index("ctx")
    section = lax.axis_index("section")
    core = lax.rem(me, 2)
    chip = me // 2
    partner = 2 * chip + 1 - core
    before = lax.rem(section + sections - 1, sections)
    after = lax.rem(section + 1, sections)

    def peer(offset):
        return paired_chip(chip, offset, chips)

    load_q = pltpu.make_async_copy(q_hbm, q_in, load_sem.at[0])
    load_g = pltpu.make_async_copy(g_hbm, g_in, load_sem.at[1])
    load_q.start()
    load_g.start()

    barrier = pltpu.get_barrier_semaphore()
    pl.semaphore_signal(barrier, inc=1, device_id=(section, partner), device_id_type=MESH)
    for o in range(1, chips):
        pl.semaphore_signal(
            barrier, inc=1, device_id=(section, 2 * peer(o) + core), device_id_type=MESH
        )
    pl.semaphore_signal(barrier, inc=1, device_id=(before, me), device_id_type=MESH)
    pl.semaphore_signal(barrier, inc=1, device_id=(after, me), device_id_type=MESH)

    load_q.wait()
    load_g.wait()
    for h in range(group):
        at = slice(h * rows, (h + 1) * rows)
        col = slice(h * head, (h + 1) * head)
        q_rows[at, :] = q_in[:, col]
        g_rows[at, :] = g_in[:, col]
        q_turned[:, at] = q_in[:, col].T
        g_turned[:, at] = g_in[:, col].T
    kv_all[me] = kv_ref[...]

    pl.semaphore_wait(barrier, chips + 2)

    def kv_copy(o):
        return pltpu.make_async_remote_copy(
            src_ref=kv_ref,
            dst_ref=kv_all.at[me],
            send_sem=kv_send_sem.at[o],
            recv_sem=kv_recv_sem.at[me],
            device_id=(section, 2 * peer(o) + core),
            device_id_type=MESH,
        )

    def kv_partner():
        return pltpu.make_async_remote_copy(
            src_ref=kv_ref,
            dst_ref=kv_all.at[me],
            send_sem=kv_send_sem.at[0],
            recv_sem=kv_recv_sem.at[me],
            device_id=(section, partner),
            device_id_type=MESH,
        )

    def kv_pass(o):
        origin = 2 * peer(o) + core
        return pltpu.make_async_remote_copy(
            src_ref=kv_all.at[origin],
            dst_ref=kv_all.at[origin],
            send_sem=kv_pass_sem.at[o],
            recv_sem=kv_recv_sem.at[origin],
            device_id=(section, partner),
            device_id_type=MESH,
        )

    def kv_arrived(origin):
        pltpu.make_async_remote_copy(
            src_ref=kv_ref,
            dst_ref=kv_all.at[origin],
            send_sem=kv_send_sem.at[0],
            recv_sem=kv_recv_sem.at[origin],
            device_id=(section, partner),
            device_id_type=MESH,
        ).wait_recv()

    kv_partner().start()
    for o in range(1, chips):
        kv_copy(o).start()

    row_ids = lax.broadcasted_iota(jnp.int32, (rows, rows), 0)
    lane_ids = lax.broadcasted_iota(jnp.int32, (rows, rows), 1)

    def place_down(block):
        first = block[rows : rows + 1, :rows].astype(jnp.float32).astype(jnp.int32)
        second = block[rows + 1 : rows + 2, :rows].astype(jnp.float32).astype(jnp.int32)
        stretch = jnp.where(row_ids < half, first, second)
        return stretch * half + lax.rem(row_ids, half)

    own = kv_ref[...]
    first = own[rows : rows + 1, :rows].astype(jnp.float32).astype(jnp.int32)
    second = own[rows + 1 : rows + 2, :rows].astype(jnp.float32).astype(jnp.int32)
    place_across = jnp.where(lane_ids < half, first, second) * half + lax.rem(lane_ids, half)

    def gather_step(o):
        there = peer(o)
        mine, other = 2 * there + core, 2 * there + 1 - core

        def first_steps():
            if isinstance(o, int) and o == 0:
                kv_arrived(partner)
            else:
                kv_arrived(mine)
                kv_pass(o).start()
                kv_arrived(other)

        if isinstance(o, int):
            first_steps()
        else:
            kv_arrived(mine)
            kv_pass(o).start()
            kv_arrived(other)
        a, b = kv_all[mine], kv_all[other]
        k = jnp.concatenate([a[:rows, :head], b[:rows, :head]], axis=0)
        v = jnp.concatenate([a[:rows, head:], b[:rows, head:]], axis=0)
        visible = jnp.concatenate(
            [place_down(a) <= place_across, place_down(b) <= place_across], axis=0
        )
        visible = jnp.concatenate([visible] * group, axis=1)
        scores = dot(k, q_turned[...], ((1,), (0,))) * (scale * LOG2E)
        dprob = dot(v, g_turned[...], ((1,), (0,)))
        scores = jnp.where(visible, scores, hidden)
        block_top = jnp.max(scores, axis=0, keepdims=True)
        if isinstance(o, int) and o == 0:
            top = block_top
            e = jnp.exp2(scores - top)
            row_total[...] = jnp.sum(e, axis=0, keepdims=True)
            row_delta[...] = jnp.sum(e * dprob, axis=0, keepdims=True)
        else:
            old = row_top[...]
            top = jnp.maximum(old, block_top)
            fading = jnp.exp2(old - top)
            e = jnp.exp2(scores - top)
            row_total[...] = row_total[...] * fading + jnp.sum(e, axis=0, keepdims=True)
            row_delta[...] = row_delta[...] * fading + jnp.sum(e * dprob, axis=0, keepdims=True)
        row_top[...] = top
        tops[o] = top
        exps[o] = e
        dprobs[o] = dprob

    gather_step(0)
    if chips <= 4:
        for o in range(1, chips):
            gather_step(o)
    else:
        lax.fori_loop(1, chips, lambda o, c: (gather_step(o), c)[1], 0)

    inverse = 1.0 / row_total[...]
    delta = row_delta[...] * inverse
    last_top = row_top[...]
    dq_turned[...] = jnp.zeros_like(dq_turned)

    def pair_copy(o):
        return pltpu.make_async_remote_copy(
            src_ref=pair_send.at[o],
            dst_ref=pair_recv.at[o],
            send_sem=pair_send_sem.at[o],
            recv_sem=pair_recv_sem.at[o],
            device_id=(section, partner),
            device_id_type=MESH,
        )

    def sum_copy(o):
        return pltpu.make_async_remote_copy(
            src_ref=sum_send.at[o],
            dst_ref=sum_recv.at[chip],
            send_sem=sum_send_sem.at[o],
            recv_sem=sum_recv_sem.at[chip],
            device_id=(section, 2 * peer(o) + core),
            device_id_type=MESH,
        )

    def grad_step(o):
        there = peer(o)
        a, b = kv_all[2 * there + core], kv_all[2 * there + 1 - core]
        k = jnp.concatenate([a[:rows, :head], b[:rows, :head]], axis=0)
        fading = jnp.exp2(tops[o] - last_top) * inverse
        weights = exps[o] * fading
        probs = weights.astype(jnp.bfloat16)
        dscore = (weights * ((dprobs[o] - delta) * scale)).astype(jnp.bfloat16)
        dk = dot(dscore, q_rows[...], ((1,), (0,)))
        dv = dot(probs, g_rows[...], ((1,), (0,)))
        part = jnp.concatenate([dk, dv], axis=1)
        pair_send[o] = part[rows:].astype(jnp.bfloat16)
        pair_copy(o).start()
        own_part[o] = part[:rows]
        dq_turned[...] += dot(k, dscore, ((0,), (0,)))

    def sum_step(o):
        pair_copy(o).wait_recv()
        sum_send[o] = (own_part[o] + pair_recv[o].astype(jnp.float32)).astype(jnp.bfloat16)
        sum_copy(o).start()

    grad_step(chips - 1)
    if chips <= 4:
        for o in reversed(range(chips - 1)):
            grad_step(o)
            sum_step(o + 1)
    else:

        def both(i, c):
            o = chips - 2 - i
            grad_step(o)
            sum_step(o + 1)
            return c

        lax.fori_loop(0, chips - 1, both, 0)

    for h in range(group):
        at = slice(h * rows, (h + 1) * rows)
        message[:, h * head : (h + 1) * head] = dq_turned[:, at].T.astype(jnp.bfloat16)

    def relay(which, columns):
        return pltpu.make_async_remote_copy(
            src_ref=message.at[:, columns],
            dst_ref=out_ref.at[:, columns],
            send_sem=relay_send_sem.at[which],
            recv_sem=relay_recv_sem.at[which],
            device_id=(before, me),
            device_id_type=MESH,
        )

    width = group * head
    relay_q = relay(0, slice(0, width))
    relay_kv = relay(1, slice(width, width + 2 * head))
    relay_q.start()

    pair_copy(0).wait_recv()
    total = own_part[0] + pair_recv[0].astype(jnp.float32)

    def take(o, total):
        there = peer(o)
        pltpu.make_async_remote_copy(
            src_ref=sum_send.at[0],
            dst_ref=sum_recv.at[there],
            send_sem=sum_send_sem.at[0],
            recv_sem=sum_recv_sem.at[there],
            device_id=(section, partner),
            device_id_type=MESH,
        ).wait_recv()
        return total + sum_recv[there].astype(jnp.float32)

    if chips <= 4:
        for o in reversed(range(1, chips)):
            total = take(o, total)
    else:
        total = lax.fori_loop(1, chips, take, total)
    message[:, width:] = total.astype(jnp.bfloat16)
    relay_kv.start()

    kv_partner().wait_send()
    pair_copy(0).wait_send()

    def finish(o):
        kv_copy(o).wait_send()
        kv_pass(o).wait_send()
        pair_copy(o).wait_send()
        sum_copy(o).wait_send()

    if chips <= 4:
        for o in range(1, chips):
            finish(o)
    else:
        lax.fori_loop(1, chips, lambda o, c: (finish(o), c)[1], 0)
    relay_q.wait()
    relay_kv.wait()


def per_device(sections, n, queries, keys, values, out_grad, stretch_ids, stash_slot):
    slot = stash_slot[0]
    q = lax.dynamic_index_in_dim(queries[0], slot, 0, keepdims=False)
    k = lax.dynamic_index_in_dim(keys[0], slot, 0, keepdims=False)
    v = lax.dynamic_index_in_dim(values[0], slot, 0, keepdims=False)
    g = out_grad[0]
    rows, head = k.shape
    width = q.shape[1]
    group = width // head
    chips = n // 2
    marks = jnp.broadcast_to(stretch_ids.astype(jnp.bfloat16)[:, None], (2, 2 * head))
    kv = jnp.concatenate(
        [jnp.concatenate([k, v], axis=1), jnp.pad(marks, ((0, 14), (0, 0)))], axis=0
    )
    bf16, f32 = jnp.bfloat16, jnp.float32
    all_rows = group * rows
    block = (chips, rows, 2 * head)
    dma = pltpu.SemaphoreType.DMA
    out = pl.pallas_call(
        functools.partial(kernel, n, sections),
        out_shape=jax.ShapeDtypeStruct((rows, width + 2 * head), bf16),
        in_specs=[
            pl.BlockSpec(memory_space=pltpu.VMEM),
            pl.BlockSpec(memory_space=pl.ANY),
            pl.BlockSpec(memory_space=pl.ANY),
        ],
        out_specs=pl.BlockSpec(memory_space=pltpu.VMEM),
        scratch_shapes=[
            pltpu.VMEM((rows, width), bf16),
            pltpu.VMEM((rows, width), bf16),
            pltpu.VMEM((all_rows, head), bf16),
            pltpu.VMEM((all_rows, head), bf16),
            pltpu.VMEM((head, all_rows), bf16),
            pltpu.VMEM((head, all_rows), bf16),
            pltpu.VMEM((n,) + kv.shape, bf16),
            pltpu.VMEM((chips, 2 * rows, all_rows), f32),
            pltpu.VMEM((chips, 2 * rows, all_rows), f32),
            pltpu.VMEM((chips, 1, all_rows), f32),
            pltpu.VMEM((1, all_rows), f32),
            pltpu.VMEM((1, all_rows), f32),
            pltpu.VMEM((1, all_rows), f32),
            pltpu.VMEM((head, all_rows), f32),
            pltpu.VMEM(block, f32),
            pltpu.VMEM(block, bf16),
            pltpu.VMEM(block, bf16),
            pltpu.VMEM(block, bf16),
            pltpu.VMEM(block, bf16),
            pltpu.VMEM((rows, width + 2 * head), bf16),
            dma((2,)),
            dma((chips,)),
            dma((chips,)),
            dma((n,)),
            dma((chips,)),
            dma((chips,)),
            dma((chips,)),
            dma((chips,)),
            dma((2,)),
            dma((2,)),
        ],
        compiler_params=pltpu.CompilerParams(
            collective_id=0, has_side_effects=True, vmem_limit_bytes=60 * 1024 * 1024
        ),
    )(kv, q, g)
    return out[None]


def solution(mesh):
    in_specs = (
        P("section", None, "ctx", None),
        P("section", None, "ctx", None),
        P("section", None, "ctx", None),
        P("section", "ctx", None),
        P("ctx"),
        P("section"),
    )
    out_specs = P("section", "ctx", None)
    body = functools.partial(per_device, mesh.shape["section"], mesh.shape["ctx"])
    return jax.shard_map(
        body, mesh=mesh, in_specs=in_specs, out_specs=out_specs, check_vma=False
    )
```

time: 98.1 us -> 34 us (0.35)
  waiting for transfers between devices: 65.3 us -> 0 us
  Pallas kernels: 0 us -> 28.6 us
  matrix products: 14.2 us -> 0 us
  starting transfers between devices: 7.24 us -> 0 us
  other arithmetic: 3.73 us -> 0.72 us
  loops' own time: 1.43 us -> 0 us
  local copies, waits for them, and re-layouts: 4.85 us -> 3.72 us
    ppermute x29 -> x0, waiting for transfers between devices: 65.3 us -> none  [passed_along(): return lax.ppermute(value, axis, pairs)]
    pallas_call x0 -> x1, Pallas kernels: none -> 28.6 us  [per_device(): pl.pallas_call(functools.partial(kernel, n, sections), out_shape=jax.Shap...]
    dot_general x56 -> x0, matrix products: 14.2 us -> none  [the longest x16 4.17 us: block_scores(): jnp.einsum('thd,cd->thc', query_rows, key_block, preferred_element_type=j...]
    ppermute x29 -> x0, starting transfers between devices: 7.24 us -> none  [passed_along(): return lax.ppermute(value, axis, pairs)]
    reduce_sum x23 -> x0, other arithmetic: 2.01 us -> none  [the longest x15 1.27 us: token_positions(): jnp.sum(jnp.where(matches, stretch_numbers[None, :], 0), axis=1)]
    another operation x2 -> x0, loops' own time: 1.43 us -> none  [the longest x1 0.85 us: per_device(): lax.scan(forward_scan, (initial, own_block), None, length=span_count - 1)]
    le x14 -> x0, other arithmetic: 1.22 us -> none  [block_scores(): visible = key_place[None, None, :] <= query_place[:, None, None]]
    unnamed x9 -> x5, local copies, waits for them, and re-layouts: 2.56 us -> 2.27 us
  transfers between devices with their start and end apart: 29 -> 0, of which waited for: 15 -> 0; matrix products, arithmetic and copies ran while one was open for 13% -> 0% of each run, Pallas kernels for 0% -> 0%
where the time goes in v1:
time: 34 us; the launch traced here: 33.8 us
  Pallas kernels  28.6 us (84%)
  local copies, waits for them, and re-layouts  3.72 us (11%)
  between operations  0.77 us (2%)
  other arithmetic  0.72 us (2%)
    pallas_call x1, Pallas kernels, per_device(): pl.pallas_call(functools.partial(kernel, n, sections), out_shape=jax.Shap...  28.6 us
    unnamed x5, local copies, waits for them, and re-layouts  2.27 us
    squeeze x1, local copies, waits for them, and re-layouts, per_device(): v = lax.dynamic_index_in_dim(values[0], slot, 0, keepdims=False)  0.78 us
    concatenate x2, other arithmetic, per_device(): jnp.concatenate([jnp.concatenate([k, v], axis=1), jnp.pad(marks, ((0, 14)...  0.72 us

profile of v1, /device:TPU:0, one launch (start us, length us, event | category | flops | bytes accessed | tf_op | source)
XLA Modules:
  0.0 33.8 jit_solution(5389572755971877163)
XLA Ops:
  0.0 0.0 copy-start
  0.7 0.0 copy-start.1
  0.8 0.6 %copy-done.1 = s32[2]{0:T(128)S(1)} copy-done((s32[2]{0:T(128)S(1)}, s32[2]{0:T(128)}, u32[]{:S(2)}) %copy-start.1) | copy-done | bytes 32
  1.4 0.8 %dynamic-slice_bitcast_fusion.1 = (bf16[128,128]{1,0:T(8,128)(2,1)S(1)}, bf16[128,128]{1,0:T(8,128)(2,1)S(1)}) fusion(bf16[1,8,128,128]{3,2,1,0:T(8,128)(2,1)} %param.8, s32[]{:T(128)S(6)} %select_n.7, bf16[1,8,128,128]{3,2,1,0:T(8,128)(2,1)} %param.7), kind=kLoop, calls=%fused_computation.2 | loop fusion | bytes 131076 | tf_op jit(solution)/shard_map/jit(dynamic_index_in_dim)/squeeze | solution.py:360
  2.2 0.7 %maximum_maximum_fusion.kv_ref = bf16[144,256]{1,0:T(8,128)(2,1)} fusion(bf16[128,128]{1,0:T(8,128)(2,1)S(1)} %get-tuple-element.5, bf16[128,128]{1,0:T(8,128)(2,1)S(1)} %get-tuple-element.6, bf16[144]{0:T(256)(128)(2,1)S(1)} %compare_select_fusion), kind=kLoop, calls=%fused_computation.1 | loop fusion | flops 221184 | bytes 139552 | tf_op jit(solution)/shard_map/concatenate | solution.py:367
  2.9 0.0 copy-done
  2.9 0.7 %dynamic-slice_bitcast_fusion.q_hbm = bf16[128,512]{1,0:T(8,128)(2,1)} fusion(bf16[1,8,128,512]{3,2,1,0:T(8,128)(2,1)S(1)} %copy-done, s32[]{:T(128)S(6)} %select_n.7), kind=kLoop, calls=%fused_computation | loop fusion | bytes 262148 | tf_op jit(solution)/shard_map/jit(dynamic_index_in_dim)/squeeze | solution.py:358
  3.6 28.6 %shard_map.64 = bf16[128,768]{1,0:T(8,128)(2,1)} custom-call(bf16[144,256]{1,0:T(8,128)(2,1)} %maximum_maximum_fusion.kv_ref, bf16[128,512]{1,0:T(8,128)(2,1)} %dynamic-slice_bitcast_fusion.q_hbm, bf16[128,512]{1,0:T(8,128)(2,1)} %bitcast.13), custom_call_target="tpu_custom_call" | custom-call | tf_op jit(solution)/shard_map/pallas_call | solution.py:374
  32.1 1.6 %copy.9 = bf16[1,128,768]{2,1,0:T(8,128)(2,1)} copy(bf16[1,128,768]{2,1,0:T(8,128)(2,1)} %bitcast.12) | data formatting | bytes 393216
  (2 shorter events, 0.0 us)
Async XLA Ops:
  0.0 2.9 %copy-start = (bf16[1,8,128,512]{3,2,1,0:T(8,128)(2,1)S(1)}, bf16[1,8,128,512]{3,2,1,0:T(8,128)(2,1)}, u32[]{:S(2)}) copy-start(bf16[1,8,128,512]{3,2,1,0:T(8,128)(2,1)} %param.6) | copy-start | bytes 3145732
  0.7 0.7 %copy-start.1 = (s32[2]{0:T(128)S(1)}, s32[2]{0:T(128)}, u32[]{:S(2)}) copy-start(s32[2]{0:T(128)} %param.10) | copy-start | bytes 28

commit v2 on v1

--- a/solution.py
+++ b/solution.py
@@ -41,12 +41,20 @@
 def kernel(
     n,
     sections,
-    kv_ref,
+    slot_hbm,
+    stretch_hbm,
     q_hbm,
+    k_hbm,
+    v_hbm,
     g_hbm,
     out_ref,
+    slot_ref,
+    stretch_ref,
     q_in,
+    k_in,
+    v_in,
     g_in,
+    kv_ref,
     q_rows,
     g_rows,
     q_turned,
@@ -79,7 +87,7 @@
     chips = n // 2
     rows = kv_ref.shape[0] - 16
     head = kv_ref.shape[1] // 2
-    group = q_hbm.shape[1] // head
+    group = g_hbm.shape[1] // head
     half = rows // 2
     scale = 1.0 / math.sqrt(head)
     me = lax.axis_index("ctx")
@@ -93,8 +101,16 @@
     def peer(offset):
         return paired_chip(chip, offset, chips)
 
-    load_q = pltpu.make_async_copy(q_hbm, q_in, load_sem.at[0])
-    load_g = pltpu.make_async_copy(g_hbm, g_in, load_sem.at[1])
+    load_k = pltpu.make_async_copy(k_hbm, k_in, load_sem.at[0])
+    load_v = pltpu.make_async_copy(v_hbm, v_in, load_sem.at[1])
+    load_q = pltpu.make_async_copy(q_hbm, q_in, load_sem.at[2])
+    load_g = pltpu.make_async_copy(g_hbm, g_in, load_sem.at[3])
+    load_slot = pltpu.make_async_copy(slot_hbm, slot_ref, load_sem.at[4])
+    load_stretch = pltpu.make_async_copy(stretch_hbm, stretch_ref, load_sem.at[5])
+    load_slot.start()
+    load_stretch.start()
+    load_k.start()
+    load_v.start()
     load_q.start()
     load_g.start()
 
@@ -107,16 +123,16 @@
     pl.semaphore_signal(barrier, inc=1, device_id=(before, me), device_id_type=MESH)
     pl.semaphore_signal(barrier, inc=1, device_id=(after, me), device_id_type=MESH)
 
-    load_q.wait()
-    load_g.wait()
-    for h in range(group):
-        at = slice(h * rows, (h + 1) * rows)
-        col = slice(h * head, (h + 1) * head)
-        q_rows[at, :] = q_in[:, col]
-        g_rows[at, :] = g_in[:, col]
-        q_turned[:, at] = q_in[:, col].T
-        g_turned[:, at] = g_in[:, col].T
-    kv_all[me] = kv_ref[...]
+    load_slot.wait()
+    load_stretch.wait()
+    slot = slot_ref[0]
+    load_k.wait()
+    load_v.wait()
+    kv_ref[:rows, :head] = k_in[slot]
+    kv_ref[:rows, head:] = v_in[slot]
+    mark_ids = lax.broadcasted_iota(jnp.int32, (16, 2 * head), 0)
+    marks = jnp.where(mark_ids == 0, stretch_ref[0], stretch_ref[1])
+    kv_ref[rows:, :] = marks.astype(jnp.float32).astype(jnp.bfloat16)
 
     pl.semaphore_wait(barrier, chips + 2)
 
@@ -164,6 +180,18 @@
     kv_partner().start()
     for o in range(1, chips):
         kv_copy(o).start()
+
+    load_q.wait()
+    load_g.wait()
+    q_own = q_in[slot]
+    for h in range(group):
+        at = slice(h * rows, (h + 1) * rows)
+        col = slice(h * head, (h + 1) * head)
+        q_rows[at, :] = q_own[:, col]
+        g_rows[at, :] = g_in[:, col]
+        q_turned[:, at] = q_own[:, col].T
+        g_turned[:, at] = g_in[:, col].T
+    kv_all[me] = kv_ref[...]
 
     row_ids = lax.broadcasted_iota(jnp.int32, (rows, rows), 0)
     lane_ids = lax.broadcasted_iota(jnp.int32, (rows, rows), 1)
@@ -354,19 +382,10 @@
 
 
 def per_device(sections, n, queries, keys, values, out_grad, stretch_ids, stash_slot):
-    slot = stash_slot[0]
-    q = lax.dynamic_index_in_dim(queries[0], slot, 0, keepdims=False)
-    k = lax.dynamic_index_in_dim(keys[0], slot, 0, keepdims=False)
-    v = lax.dynamic_index_in_dim(values[0], slot, 0, keepdims=False)
-    g = out_grad[0]
-    rows, head = k.shape
-    width = q.shape[1]
+    slots, rows, head = keys.shape[1:]
+    width = queries.shape[3]
     group = width // head
     chips = n // 2
-    marks = jnp.broadcast_to(stretch_ids.astype(jnp.bfloat16)[:, None], (2, 2 * head))
-    kv = jnp.concatenate(
-        [jnp.concatenate([k, v], axis=1), jnp.pad(marks, ((0, 14), (0, 0)))], axis=0
-    )
     bf16, f32 = jnp.bfloat16, jnp.float32
     all_rows = group * rows
     block = (chips, rows, 2 * head)
@@ -375,19 +394,27 @@
         functools.partial(kernel, n, sections),
         out_shape=jax.ShapeDtypeStruct((rows, width + 2 * head), bf16),
         in_specs=[
-            pl.BlockSpec(memory_space=pltpu.VMEM),
-            pl.BlockSpec(memory_space=pl.ANY),
-            pl.BlockSpec(memory_space=pl.ANY),
+            pl.BlockSpec(memory_space=pltpu.HBM),
+            pl.BlockSpec(memory_space=pltpu.HBM),
+            pl.BlockSpec(memory_space=pltpu.HBM),
+            pl.BlockSpec(memory_space=pltpu.HBM),
+            pl.BlockSpec(memory_space=pltpu.HBM),
+            pl.BlockSpec(memory_space=pltpu.HBM),
         ],
-        out_specs=pl.BlockSpec(memory_space=pltpu.VMEM),
+        out_specs=pl.BlockSpec(memory_space=pl.ANY),
         scratch_shapes=[
+            pltpu.SMEM((1,), jnp.int32),
+            pltpu.SMEM((2,), jnp.int32),
+            pltpu.VMEM((slots, rows, width), bf16),
+            pltpu.VMEM((slots, rows, head), bf16),
+            pltpu.VMEM((slots, rows, head), bf16),
             pltpu.VMEM((rows, width), bf16),
-            pltpu.VMEM((rows, width), bf16),
+            pltpu.VMEM((rows + 16, 2 * head), bf16),
             pltpu.VMEM((all_rows, head), bf16),
             pltpu.VMEM((all_rows, head), bf16),
             pltpu.VMEM((head, all_rows), bf16),
             pltpu.VMEM((head, all_rows), bf16),
-            pltpu.VMEM((n,) + kv.shape, bf16),
+            pltpu.VMEM((n, rows + 16, 2 * head), bf16),
             pltpu.VMEM((chips, 2 * rows, all_rows), f32),
             pltpu.VMEM((chips, 2 * rows, all_rows), f32),
             pltpu.VMEM((chips, 1, all_rows), f32),
@@ -401,7 +428,7 @@
             pltpu.VMEM(block, bf16),
             pltpu.VMEM(block, bf16),
             pltpu.VMEM((rows, width + 2 * head), bf16),
-            dma((2,)),
+            dma((6,)),
             dma((chips,)),
             dma((chips,)),
             dma((n,)),
@@ -413,9 +440,9 @@
             dma((2,)),
         ],
         compiler_params=pltpu.CompilerParams(
-            collective_id=0, has_side_effects=True, vmem_limit_bytes=60 * 1024 * 1024
+            collective_id=0, has_side_effects=True, vmem_limit_bytes=67043328
         ),
-    )(kv, q, g)
+    )(stash_slot, stretch_ids, queries[0], keys[0], values[0], out_grad[0])
     return out[None]
 
 

time: 34 us -> 29.7 us (0.87)
  local copies, waits for them, and re-layouts: 3.72 us -> 1.62 us
  Pallas kernels: 28.6 us -> 27.2 us
  other arithmetic: 0.72 us -> 0 us
    squeeze x2 -> x0, local copies, waits for them, and re-layouts: 1.45 us -> none  [the longest x1 0.78 us: per_device(): v = lax.dynamic_index_in_dim(values[0], slot, 0, keepdims=False)]
    pallas_call x1, Pallas kernels: 28.6 us -> 27.2 us  [per_device(): pl.pallas_call(functools.partial(kernel, n, sections), out_shape=jax.Shap...]
    concatenate x2 -> x0, other arithmetic: 0.72 us -> none  [per_device(): jnp.concatenate([jnp.concatenate([k, v], axis=1), jnp.pad(marks, ((0, 14)...]
    unnamed x5 -> x1, local copies, waits for them, and re-layouts: 2.27 us -> 1.62 us
where the time goes in v2:
time: 29.7 us; the launch traced here: 29.5 us
  Pallas kernels  27.2 us (92%)
  local copies, waits for them, and re-layouts  1.62 us (5%)
  between operations  0.66 us (2%)
    pallas_call x1, Pallas kernels, per_device(): pl.pallas_call(functools.partial(kernel, n, sections), out_shape=jax.Shap...  27.2 us
    unnamed x1, local copies, waits for them, and re-layouts  1.62 us

profile of v2, /device:TPU:0, one launch (start us, length us, event | category | flops | bytes accessed | tf_op | source)
XLA Modules:
  0.0 29.5 jit_solution(2593151108383378628)
XLA Ops:
  0.7 27.2 %shard_map.64 = bf16[128,768]{1,0:T(8,128)(2,1)} custom-call(s32[1]{0:T(128)S(6)} %copy.8.slot_hbm, s32[2]{0:T(128)} %stretch_hbm.1, bf16[8,128,512]{2,1,0:T(8,128)(2,1)} %bitcast.5, bf16[8,128,128]{2,1,0:T(8,128)(2,1)} %bitcast.7, bf16[8,128,128]{2,1,0:T(8,128)(2,1)} %bitcast.8, bf16[128,512]{1,0:T(8,128)(2,1)} %bitcast.9), custom_call_target="tpu_custom_call" | custom-call | tf_op jit(solution)/shard_map/pallas_call | solution.py:393
  27.9 1.6 %copy.9 = bf16[1,128,768]{2,1,0:T(8,128)(2,1)} copy(bf16[1,128,768]{2,1,0:T(8,128)(2,1)} %bitcast.6) | data formatting | bytes 393216

commit v3 on v2

--- a/solution.py
+++ b/solution.py
@@ -72,7 +72,11 @@
     pair_recv,
     sum_send,
     sum_recv,
+    far_recv,
     message,
+    near_sum,
+    relayed,
+    out_kv,
     load_sem,
     kv_send_sem,
     kv_pass_sem,
@@ -81,6 +85,7 @@
     pair_recv_sem,
     sum_send_sem,
     sum_recv_sem,
+    far_recv_sem,
     relay_send_sem,
     relay_recv_sem,
 ):
@@ -101,6 +106,8 @@
     def peer(offset):
         return paired_chip(chip, offset, chips)
 
+    far = tuple(range(max(chips - 2, 1), chips))
+
     load_k = pltpu.make_async_copy(k_hbm, k_in, load_sem.at[0])
     load_v = pltpu.make_async_copy(v_hbm, v_in, load_sem.at[1])
     load_q = pltpu.make_async_copy(q_hbm, q_in, load_sem.at[2])
@@ -120,8 +127,11 @@
         pl.semaphore_signal(
             barrier, inc=1, device_id=(section, 2 * peer(o) + core), device_id_type=MESH
         )
-    pl.semaphore_signal(barrier, inc=1, device_id=(before, me), device_id_type=MESH)
     pl.semaphore_signal(barrier, inc=1, device_id=(after, me), device_id_type=MESH)
+    for o in far:
+        pl.semaphore_signal(
+            barrier, inc=1, device_id=(after, 2 * peer(o) + core), device_id_type=MESH
+        )
 
     load_slot.wait()
     load_stretch.wait()
@@ -134,7 +144,7 @@
     marks = jnp.where(mark_ids == 0, stretch_ref[0], stretch_ref[1])
     kv_ref[rows:, :] = marks.astype(jnp.float32).astype(jnp.bfloat16)
 
-    pl.semaphore_wait(barrier, chips + 2)
+    pl.semaphore_wait(barrier, chips + 1 + len(far))
 
     def kv_copy(o):
         return pltpu.make_async_remote_copy(
@@ -276,6 +286,15 @@
         )
 
     def sum_copy(o):
+        if isinstance(o, int) and o in far:
+            return pltpu.make_async_remote_copy(
+                src_ref=sum_send.at[o],
+                dst_ref=far_recv.at[o - far[0]],
+                send_sem=sum_send_sem.at[o],
+                recv_sem=far_recv_sem.at[o - far[0]],
+                device_id=(before, 2 * peer(o) + core),
+                device_id_type=MESH,
+            )
         return pltpu.make_async_remote_copy(
             src_ref=sum_send.at[o],
             dst_ref=sum_recv.at[chip],
@@ -306,38 +325,47 @@
         sum_send[o] = (own_part[o] + pair_recv[o].astype(jnp.float32)).astype(jnp.bfloat16)
         sum_copy(o).start()
 
-    grad_step(chips - 1)
     if chips <= 4:
-        for o in reversed(range(chips - 1)):
+        order = (3, 2, 1, 0) if chips == 4 else tuple(reversed(range(chips)))
+        for place, o in enumerate(order):
             grad_step(o)
-            sum_step(o + 1)
+            if place:
+                sum_step(order[place - 1])
     else:
+        grad_step(chips - 1)
+        for o in reversed(far):
+            grad_step(o - 1)
+            sum_step(o)
 
         def both(i, c):
-            o = chips - 2 - i
+            o = far[0] - 2 - i
             grad_step(o)
             sum_step(o + 1)
             return c
 
-        lax.fori_loop(0, chips - 1, both, 0)
+        lax.fori_loop(0, far[0] - 1, both, 0)
 
     for h in range(group):
         at = slice(h * rows, (h + 1) * rows)
         message[:, h * head : (h + 1) * head] = dq_turned[:, at].T.astype(jnp.bfloat16)
 
-    def relay(which, columns):
-        return pltpu.make_async_remote_copy(
-            src_ref=message.at[:, columns],
-            dst_ref=out_ref.at[:, columns],
-            send_sem=relay_send_sem.at[which],
-            recv_sem=relay_recv_sem.at[which],
-            device_id=(before, me),
-            device_id_type=MESH,
-        )
-
     width = group * head
-    relay_q = relay(0, slice(0, width))
-    relay_kv = relay(1, slice(width, width + 2 * head))
+    relay_q = pltpu.make_async_remote_copy(
+        src_ref=message,
+        dst_ref=out_ref.at[:, :width],
+        send_sem=relay_send_sem.at[0],
+        recv_sem=relay_recv_sem.at[0],
+        device_id=(before, me),
+        device_id_type=MESH,
+    )
+    relay_kv = pltpu.make_async_remote_copy(
+        src_ref=near_sum,
+        dst_ref=relayed,
+        send_sem=relay_send_sem.at[1],
+        recv_sem=relay_recv_sem.at[1],
+        device_id=(before, me),
+        device_id_type=MESH,
+    )
     relay_q.start()
 
     pair_copy(0).wait_recv()
@@ -356,11 +384,11 @@
         return total + sum_recv[there].astype(jnp.float32)
 
     if chips <= 4:
-        for o in reversed(range(1, chips)):
+        for o in range(1, far[0]):
             total = take(o, total)
     else:
-        total = lax.fori_loop(1, chips, take, total)
-    message[:, width:] = total.astype(jnp.bfloat16)
+        total = lax.fori_loop(1, far[0], take, total)
+    near_sum[...] = total.astype(jnp.bfloat16)
     relay_kv.start()
 
     kv_partner().wait_send()
@@ -372,13 +400,21 @@
         pair_copy(o).wait_send()
         sum_copy(o).wait_send()
 
-    if chips <= 4:
-        for o in range(1, chips):
-            finish(o)
-    else:
-        lax.fori_loop(1, chips, lambda o, c: (finish(o), c)[1], 0)
+    if chips > 4:
+        lax.fori_loop(1, far[0], lambda o, c: (finish(o), c)[1], 0)
+    for o in far if chips > 4 else range(1, chips):
+        finish(o)
+
+    relay_kv.wait()
+    total = relayed[...].astype(jnp.float32)
+    for o in far:
+        sum_copy(o).wait_recv()
+        total = total + far_recv[o - far[0]].astype(jnp.float32)
+    out_kv[...] = total.astype(jnp.bfloat16)
+    store = pltpu.make_async_copy(out_kv, out_ref.at[:, width:], load_sem.at[0])
+    store.start()
     relay_q.wait()
-    relay_kv.wait()
+    store.wait()
 
 
 def per_device(sections, n, queries, keys, values, out_grad, stretch_ids, stash_slot):
@@ -427,7 +463,11 @@
             pltpu.VMEM(block, bf16),
             pltpu.VMEM(block, bf16),
             pltpu.VMEM(block, bf16),
-            pltpu.VMEM((rows, width + 2 * head), bf16),
+            pltpu.VMEM((2, rows, 2 * head), bf16),
+            pltpu.VMEM((rows, width), bf16),
+            pltpu.VMEM((rows, 2 * head), bf16),
+            pltpu.VMEM((rows, 2 * head), bf16),
+            pltpu.VMEM((rows, 2 * head), bf16),
             dma((6,)),
             dma((chips,)),
             dma((chips,)),
@@ -436,6 +476,7 @@
             dma((chips,)),
             dma((chips,)),
             dma((chips,)),
+            dma((2,)),
             dma((2,)),
             dma((2,)),
         ],

time: 29.7 us -> 28.9 us (0.973)
  Pallas kernels: 27.2 us -> 26.5 us
    pallas_call x1, Pallas kernels: 27.2 us -> 26.5 us  [per_device(): pl.pallas_call(functools.partial(kernel, n, sections), out_shape=jax.Shap...]
where the time goes in v3:
time: 28.9 us; the launch traced here: 28.7 us
  Pallas kernels  26.5 us (92%)
  local copies, waits for them, and re-layouts  1.62 us (6%)
  between operations  0.66 us (2%)
    pallas_call x1, Pallas kernels, per_device(): pl.pallas_call(functools.partial(kernel, n, sections), out_shape=jax.Shap...  26.5 us
    unnamed x1, local copies, waits for them, and re-layouts  1.62 us

profile of v3, /device:TPU:0, one launch (start us, length us, event | category | flops | bytes accessed | tf_op | source)
XLA Modules:
  0.0 28.7 jit_solution(6125943560738671185)
XLA Ops:
  0.7 26.5 %shard_map.64 = bf16[128,768]{1,0:T(8,128)(2,1)} custom-call(s32[1]{0:T(128)S(6)} %copy.8.slot_hbm, s32[2]{0:T(128)} %stretch_hbm.1, bf16[8,128,512]{2,1,0:T(8,128)(2,1)} %bitcast.5, bf16[8,128,128]{2,1,0:T(8,128)(2,1)} %bitcast.7, bf16[8,128,128]{2,1,0:T(8,128)(2,1)} %bitcast.8, bf16[128,512]{1,0:T(8,128)(2,1)} %bitcast.9), custom_call_target="tpu_custom_call" | custom-call | tf_op jit(solution)/shard_map/pallas_call | solution.py:429
  27.1 1.6 %copy.9 = bf16[1,128,768]{2,1,0:T(8,128)(2,1)} copy(bf16[1,128,768]{2,1,0:T(8,128)(2,1)} %bitcast.6) | data formatting | bytes 393216

commit v4 on v3

--- a/solution.py
+++ b/solution.py
@@ -428,7 +428,7 @@
     dma = pltpu.SemaphoreType.DMA
     out = pl.pallas_call(
         functools.partial(kernel, n, sections),
-        out_shape=jax.ShapeDtypeStruct((rows, width + 2 * head), bf16),
+        out_shape=pltpu.VMEM((rows, width + 2 * head), bf16),
         in_specs=[
             pl.BlockSpec(memory_space=pltpu.HBM),
             pl.BlockSpec(memory_space=pltpu.HBM),
@@ -481,7 +481,7 @@
             dma((2,)),
         ],
         compiler_params=pltpu.CompilerParams(
-            collective_id=0, has_side_effects=True, vmem_limit_bytes=67043328
+            collective_id=0, has_side_effects=True, vmem_limit_bytes=67043328 - (3 << 20)
         ),
     )(stash_slot, stretch_ids, queries[0], keys[0], values[0], out_grad[0])
     return out[None]

time: 28.9 us -> 27.3 us (0.945)
  local copies, waits for them, and re-layouts: 1.62 us -> 0.68 us
  Pallas kernels: 26.5 us -> 25.8 us
    unnamed x1, local copies, waits for them, and re-layouts: 1.62 us -> 0.68 us
    pallas_call x1, Pallas kernels: 26.5 us -> 25.8 us  [per_device(): pl.pallas_call(functools.partial(kernel, n, sections), out_shape=pltpu.VM...]
where the time goes in v4:
time: 27.3 us; the launch traced here: 27.2 us
  Pallas kernels  25.8 us (95%)
  local copies, waits for them, and re-layouts  0.68 us (2%)
  between operations  0.66 us (2%)
    pallas_call x1, Pallas kernels, per_device(): pl.pallas_call(functools.partial(kernel, n, sections), out_shape=pltpu.VM...  25.8 us
    unnamed x1, local copies, waits for them, and re-layouts  0.68 us

profile of v4, /device:TPU:0, one launch (start us, length us, event | category | flops | bytes accessed | tf_op | source)
XLA Modules:
  0.0 27.2 jit_solution(3184948775651715614)
XLA Ops:
  0.7 25.8 %shard_map.64 = bf16[128,768]{1,0:T(8,128)(2,1)S(1)} custom-call(s32[1]{0:T(128)S(6)} %copy.9.slot_hbm, s32[2]{0:T(128)} %stretch_hbm.1, bf16[8,128,512]{2,1,0:T(8,128)(2,1)} %bitcast.6, bf16[8,128,128]{2,1,0:T(8,128)(2,1)} %bitcast.7, bf16[8,128,128]{2,1,0:T(8,128)(2,1)} %bitcast.8, bf16[128,512]{1,0:T(8,128)(2,1)} %bitcast.9), custom_call_target="tpu_custom_call" | custom-call | tf_op jit(solution)/shard_map/pallas_call | solution.py:429
  26.5 0.7 %copy.8 = bf16[1,128,768]{2,1,0:T(8,128)(2,1)} copy(bf16[1,128,768]{2,1,0:T(8,128)(2,1)S(1)} %bitcast.5) | data formatting | bytes 393216
